TPU v7x, 32 devices: a whole 2x2x4 slice. The times are simulated.
32 devices in a mesh: model: 4 (over z), data: 2 (over y), stage: 4 (over x, core).
Axes of the slice: x: 2, y: 2, z: 4, core: 2. Of those that a mesh axis runs over, the one named last changes fastest.
Arguments:
- w_up: float32 [4, 1024, 4096], P('stage', None, 'model')
- w_down: float32 [4, 4096, 1024], P('stage', 'model')
- m_up: float32 [4, 1024, 4096], P('stage', None, 'model')
- m_down: float32 [4, 4096, 1024], P('stage', 'model')
- v_up: float32 [4, 1024, 4096], P('stage', None, 'model')
- v_down: float32 [4, 4096, 1024], P('stage', 'model')
- g_up: float32 [2, 4, 1024, 4096], P('data', 'stage', None, 'model')
- g_down: float32 [2, 4, 4096, 1024], P('data', 'stage', 'model')
- acts_last: bfloat16 [4, 256, 1024], P('stage', 'data')
- grad_out: bfloat16 [256, 1024], P('data')
- x_next: bfloat16 [3, 256, 1024], P(None, 'data')
- learn_rate: float32 [1], replicated
- max_norm: float32 [1], replicated
Outputs:
- output 1: float32 [4, 1024, 4096], P('stage', None, 'model')
- output 2: float32 [4, 4096, 1024], P('stage', 'model')
- output 3: float32 [4, 1024, 4096], P('stage', None, 'model')
- output 4: float32 [4, 4096, 1024], P('stage', 'model')
- output 5: float32 [4, 1024, 4096], P('stage', None, 'model')
- output 6: float32 [4, 4096, 1024], P('stage', 'model')
- output 7: bfloat16 [3, 256, 1024], P(None, 'data')
All inputs are finite; a program needn't handle non-finite values.
Results may differ from a plain program's by a relative error of at most 0.00840855.
Values are sent between devices in bfloat16 or wider.
A program may use at most 1 GiB of HBM per device.

v0:
```python
import jax
import jax.numpy as jnp
from jax import lax
from jax.sharding import PartitionSpec as P

ADAM_STEP = 10
BETA_ONE = 0.9
BETA_TWO = 0.95
ADAM_EPS = 1e-8
WEIGHT_DECAY = 0.1
NORM_EPS = 1e-6
CONTRACT_LAST = (((1,), (1,)), ((), ()))
CONTRACT_FIRST = (((0,), (0,)), ((), ()))


def gelu_vjp(pre_act, upstream):
    pull_back = jax.vjp(jax.nn.gelu, pre_act)[1]
    return pull_back(upstream)[0]


def adamw_update(weight, moment_one, moment_two, grad_step, step_rate):
    mom_new = BETA_ONE * moment_one + (1.0 - BETA_ONE) * grad_step
    sec_new = BETA_TWO * moment_two + (1.0 - BETA_TWO) * grad_step * grad_step
    one_corr = 1.0 - BETA_ONE ** ADAM_STEP
    two_corr = 1.0 - BETA_TWO ** ADAM_STEP
    direction = (mom_new / one_corr) / (jnp.sqrt(sec_new / two_corr) + ADAM_EPS)
    weight_new = weight - step_rate * (direction + WEIGHT_DECAY * weight)
    return weight_new, mom_new, sec_new


def solution(mesh):
    n_stage = mesh.shape['stage']
    n_data = mesh.shape['data']
    down_perm = [(sender, sender - 1) for sender in range(1, n_stage)]
    up_perm = [(sender, sender + 1) for sender in range(n_stage - 1)]
    up_spec = P('stage', None, 'model')
    down_spec = P('stage', 'model', None)
    row_spec = P(None, 'data', None)
    in_specs = (up_spec, down_spec, up_spec, down_spec, up_spec, down_spec, P('data', 'stage', None, 'model'), P('data', 'stage', 'model', None), P('stage', 'data', None), P('data', None), row_spec, P(None), P(None))
    out_specs = (up_spec, down_spec, up_spec, down_spec, up_spec, down_spec, row_spec)

    def device_step(w_up, w_down, m_up, m_down, v_up, v_down, g_up, g_down, acts_last, grad_out, x_next, learn_rate, max_norm):
        stage_id = lax.axis_index('stage')
        acts_in = acts_last[0]
        up_bf = w_up[0].astype(jnp.bfloat16)
        down_bf = w_down[0].astype(jnp.bfloat16)
        row_count, d_model = acts_in.shape
        ff_local = up_bf.shape[1]
        n_micro = x_next.shape[0]

        def back_core(upstream):
            pre_act = jnp.dot(acts_in, up_bf, preferred_element_type=jnp.float32)
            hidden = jax.nn.gelu(pre_act).astype(jnp.bfloat16)
            grad_hid = lax.dot_general(upstream, down_bf, CONTRACT_LAST, preferred_element_type=jnp.float32)
            grad_pre = gelu_vjp(pre_act, grad_hid).astype(jnp.bfloat16)
            return hidden, grad_pre

        def back_send(state_in):
            hidden, grad_pre = back_core(state_in[0])
            part_sum = lax.dot_general(grad_pre, up_bf, CONTRACT_LAST, preferred_element_type=jnp.float32)
            return hidden, grad_pre, state_in[0], part_sum

        def hold_send(state_in):
            return state_in[1], state_in[2], state_in[3], jnp.zeros((row_count, d_model), jnp.float32)

        def back_keep(state_in):
            hidden, grad_pre = back_core(state_in[0])
            return hidden, grad_pre, state_in[0]

        def hold_keep(state_in):
            return state_in[1], state_in[2], state_in[3]

        upstream = grad_out
        keep_hid = jnp.zeros((row_count, ff_local), jnp.bfloat16)
        keep_pre = jnp.zeros((row_count, ff_local), jnp.bfloat16)
        keep_up = grad_out
        for step_idx in range(n_stage - 1):
            active = stage_id == n_stage - 1 - step_idx
            keep_hid, keep_pre, keep_up, part_sum = lax.cond(active, back_send, hold_send, (upstream, keep_hid, keep_pre, keep_up))
            summed = lax.psum(part_sum, 'model')
            grad_in = (upstream.astype(jnp.float32) + summed).astype(jnp.bfloat16)
            upstream = lax.ppermute(grad_in, 'stage', down_perm)
        keep_hid, keep_pre, keep_up = lax.cond(stage_id == 0, back_keep, hold_keep, (upstream, keep_hid, keep_pre, keep_up))

        grad_down = lax.dot_general(keep_hid, keep_up, CONTRACT_FIRST, preferred_element_type=jnp.float32)
        grad_up = lax.dot_general(acts_in, keep_pre, CONTRACT_FIRST, preferred_element_type=jnp.float32)
        mean_up = lax.psum(g_up[0, 0] + grad_up, 'data') / n_data
        mean_down = lax.psum(g_down[0, 0] + grad_down, 'data') / n_data
        local_sq = lax.psum(jnp.sum(mean_up * mean_up) + jnp.sum(mean_down * mean_down), 'model')
        norm_acc = local_sq
        for step_idx in range(n_stage - 1):
            incoming = lax.ppermute(norm_acc, 'stage', down_perm)
            norm_acc = jnp.where(stage_id == n_stage - 2 - step_idx, local_sq + incoming, norm_acc)
        clip_cur = jnp.minimum(1.0, max_norm[0] / (jnp.sqrt(norm_acc) + NORM_EPS))
        step_rate = learn_rate[0]

        def apply_update(state_in):
            clip_now = state_in[1]
            up_w, up_m, up_v = adamw_update(w_up[0], m_up[0], v_up[0], clip_now * mean_up, step_rate)
            down_w, down_m, down_v = adamw_update(w_down[0], m_down[0], v_down[0], clip_now * mean_down, step_rate)
            return (up_w, down_w, up_m, down_m, up_v, down_v, up_w.astype(jnp.bfloat16), down_w.astype(jnp.bfloat16))

        def keep_state(state_in):
            return state_in[0]

        def fwd_local(state_in):
            acts_cur, up_new_bf, down_new_bf = state_in
            pre_act = jnp.dot(acts_cur, up_new_bf, preferred_element_type=jnp.float32)
            hidden = jax.nn.gelu(pre_act).astype(jnp.bfloat16)
            return jnp.dot(hidden, down_new_bf, preferred_element_type=jnp.float32)

        def fwd_idle(state_in):
            return jnp.zeros((row_count, d_model), jnp.float32)

        opt_state = (w_up[0], w_down[0], m_up[0], m_down[0], v_up[0], v_down[0], up_bf, down_bf)
        acts_cur = x_next[0]
        finished = []
        for step_idx in range(n_micro + n_stage - 1):
            if step_idx < n_stage:
                opt_state = lax.cond(stage_id == step_idx, apply_update, keep_state, (opt_state, clip_cur))
            if 0 < step_idx < n_micro:
                acts_cur = jnp.where(stage_id == 0, x_next[step_idx], acts_cur)
            micro_idx = step_idx - stage_id
            is_busy = (micro_idx >= 0) & (micro_idx < n_micro)
            branch = lax.cond(is_busy, fwd_local, fwd_idle, (acts_cur, opt_state[6], opt_state[7]))
            summed = lax.psum(branch, 'model')
            acts_out = (acts_cur.astype(jnp.float32) + summed).astype(jnp.bfloat16)
            if step_idx >= n_stage - 1:
                finished.append(acts_out)
            if step_idx < n_micro + n_stage - 2:
                acts_cur = lax.ppermute(acts_out, 'stage', up_perm)
            if step_idx < n_stage - 1:
                clip_cur = lax.ppermute(clip_cur, 'stage', up_perm)
        y_local = jnp.stack(finished)
        y_next = lax.psum(jnp.where(stage_id == n_stage - 1, y_local, jnp.zeros_like(y_local)), 'stage')
        return (opt_state[0][None], opt_state[1][None], opt_state[2][None], opt_state[3][None], opt_state[4][None], opt_state[5][None], y_next)

    return jax.shard_map(device_step, mesh=mesh, in_specs=in_specs, out_specs=out_specs, check_vma=False)
```

profile of v0, /device:TPU:7, one launch (start us, length us, event | category | flops | bytes accessed | tf_op | source)
XLA Modules:
  0.0 898.6 jit_solution(9596167457095429306)
XLA Ops:
  7.2 5.5 bitcast_convert_fusion
  12.8 6.4 conditional.14
  13.6 3.0 fusion.6
  16.6 2.5 fusion.193
  20.0 38.6 %all-reduce.13.cloned.1.call-done = f32[128,1024]{1,0:T(8,128)} async-done(((f32[128,1024]{1,0:T(8,128)}), f32[128,1024]{1,0:T(8,128)}) %all-reduce.13.cloned.1.call-update) | async-done | bytes 524304 | tf_op jit(solution)/shard_map/psum | solution.py:80
  59.7 3.4 collective-permute-start
  65.1 46.8 %all-reduce.15.cloned.1.call-done = f32[128,1024]{1,0:T(8,128)} async-done(((f32[128,1024]{1,0:T(8,128)}), f32[128,1024]{1,0:T(8,128)}) %all-reduce.15.cloned.1.call-update) | async-done | bytes 524304 | tf_op jit(solution)/shard_map/psum | solution.py:80
  113.0 3.4 collective-permute-start.1
  118.5 46.7 %all-reduce.17.cloned.1.call-done = f32[128,1024]{1,0:T(8,128)} async-done(((f32[128,1024]{1,0:T(8,128)}), f32[128,1024]{1,0:T(8,128)}) %all-reduce.17.cloned.1.call-update) | async-done | bytes 524304 | tf_op jit(solution)/shard_map/psum | solution.py:80
  166.3 3.4 collective-permute-start.2
  169.7 5.3 copy.21
  175.1 5.3 copy.20
  180.4 5.2 bitcast_add_fusion.9
  185.6 2.8 bitcast_add_fusion.8
  190.3 196.8 %all-reduce.33.cloned.1.call-done = (f32[1024,1024]{0,1:T(8,128)}, f32[1024,1024]{0,1:T(8,128)}) async-done(((f32[1024,1024]{0,1:T(8,128)}, f32[1024,1024]{0,1:T(8,128)}), (f32[1024,1024]{0,1:T(8,128)}, f32[1024,1024]{0,1:T(8,128)})) %all-reduce.33.cloned.1.call-update) | async-done | bytes 8388624 | tf_op jit(solution)/shard_map/psum | solution.py:87
  387.1 6.0 broadcast_multiply_fusion
  393.1 3.6 broadcast_multiply_fusion.1
  398.0 10.2 %psum.96 = f32[]{:T(128)} all-reduce(f32[]{:T(128)S(6)} %add.247), channel_id=1, replica_groups=mesh['model'=4,'data'=2,'stage'=4] {'model'}, use_global_device_ids=true, to_apply=%region_15.0 | all-reduce | flops 1 | bytes 8 | tf_op jit(solution)/shard_map/psum | solution.py:89
  408.2 5.4 collective-permute-start.3
  415.8 3.2 collective-permute-start.4
  420.4 4.9 collective-permute-start.5
  426.7 21.8 %conditional.18 = (f32[1024,1024]{1,0:T(8,128)}, f32[1024,1024]{1,0:T(8,128)}, f32[1024,1024]{1,0:T(8,128)}, f32[1024,1024]{1,0:T(8,128)}, f32[1024,1024]{1,0:T(...) conditional(s32[]{:T(128)} %convert_element_type.163, ...), branch_computations={%region_16.17_spmd, %region_17.18_spmd} | conditional | flops 35651584 | bytes 134217952 | solution.py:120
  426.7 4.9 copy.65
  431.7 2.1 copy.66
  435.4 2.1 copy.67
  439.1 2.1 copy.68
  449.4 51.2 %all-reduce.19.cloned.1.call-done = f32[128,1024]{1,0:T(8,128)} async-done(((f32[128,1024]{1,0:T(8,128)}), f32[128,1024]{1,0:T(8,128)}) %all-reduce.19.cloned.1.call-update) | async-done | bytes 524304 | tf_op jit(solution)/shard_map/psum | solution.py:126
  504.3 3.3 collective-permute-done.6
  509.3 75.9 %all-reduce.21.cloned.1.call-done = f32[128,1024]{1,0:T(8,128)} async-done(((f32[128,1024]{1,0:T(8,128)}), f32[128,1024]{1,0:T(8,128)}) %all-reduce.21.cloned.1.call-update) | async-done | bytes 524304 | tf_op jit(solution)/shard_map/psum | solution.py:126
  589.0 3.3 collective-permute-done.7
  593.9 78.0 %all-reduce.23.cloned.1.call-done = f32[128,1024]{1,0:T(8,128)} async-done(((f32[128,1024]{1,0:T(8,128)}), f32[128,1024]{1,0:T(8,128)}) %all-reduce.23.cloned.1.call-update) | async-done | bytes 524304 | tf_op jit(solution)/shard_map/psum | solution.py:126
  675.7 3.3 collective-permute-done.8
  679.0 35.3 %conditional.21 = (bf16[1024,1024]{1,0:T(8,128)(2,1)}, bf16[1024,1024]{1,0:T(8,128)(2,1)S(1)}, f32[1,1024,1024]{2,1,0:T(8,128)}, f32[1,1024,1024]{2,1,0:T(8,128)...) conditional(s32[]{:T(128)} %convert_element_type.160, ...), branch_computations={%region_22.23_spmd, %region_23.24_spmd} | conditional | flops 35651584 | bytes 79691848 | solution.py:120
  679.0 5.3 copy.29
  684.4 5.4 copy.30
  689.8 24.5 %fusion.178 = (bf16[1024,1024]{1,0:T(8,128)(2,1)S(1)}, f32[1024,1024]{1,0:T(8,128)}, f32[1,1024,1024]{2,1,0:T(8,128)}, f32[1,1024,1024]{2,1,0:T(8,128)}, f32[1,1...) fusion(f32[1,1024,1024]{2,1,0:T(8,128)} %get-tuple-element.332, ...), kind=kLoop, calls=%fused_computation.237 | loop fusion | flops 35651584 | bytes 62914568 | tf_op jit(solution)/shard_map/cond/branch_1_fun/convert_element_type | solution.py:101
  714.3 2.5 conditional.25
  714.3 2.4 fusion.118
  717.6 37.2 %all-reduce.25.cloned.1.call-done = f32[128,1024]{1,0:T(8,128)} async-done(((f32[128,1024]{1,0:T(8,128)}), f32[128,1024]{1,0:T(8,128)}) %all-reduce.25.cloned.1.call-update) | async-done | bytes 524304 | tf_op jit(solution)/shard_map/psum | solution.py:126
  757.2 3.1 collective-permute-done.12
  760.3 2.4 conditional.26
  760.3 2.4 fusion.136
  763.6 41.7 %all-reduce.27.cloned.1.call-done = f32[128,1024]{1,0:T(8,128)} async-done(((f32[128,1024]{1,0:T(8,128)}), f32[128,1024]{1,0:T(8,128)}) %all-reduce.27.cloned.1.call-update) | async-done | bytes 524304 | tf_op jit(solution)/shard_map/psum | solution.py:126
  807.7 3.1 collective-permute-done.13
  810.8 2.4 conditional.27
  810.8 2.4 fusion.154
  814.1 39.3 %all-reduce.29.cloned.1.call-done = f32[128,1024]{1,0:T(8,128)} async-done(((f32[128,1024]{1,0:T(8,128)}), f32[128,1024]{1,0:T(8,128)}) %all-reduce.29.cloned.1.call-update) | async-done | bytes 524304 | tf_op jit(solution)/shard_map/psum | solution.py:126
  855.5 34.4 %all-reduce.31.cloned.1.call-done = bf16[3,128,1024]{2,1,0:T(8,128)(2,1)} async-done(((bf16[3,128,1024]{2,1,0:T(8,128)(2,1)}), bf16[3,128,1024]{2,1,0:T(8,128)(2,1)}) %all-reduce.31.cloned.1.call-update) | async-done | bytes 786448 | tf_op jit(solution)/shard_map/psum | solution.py:135
  (107 shorter events, 47.8 us)
Async XLA Ops:
  7.2 51.4 %all-reduce.13.cloned.1.call-start = ((), (), s32[]{:S(2)}) async-start(), calls=%async_computation | async-start | bytes 1048576 | tf_op jit(solution)/shard_map/psum | solution.py:80
  7.2 5.5 copy-start.7
  7.2 5.5 copy-start.18
  19.1 0.8 copy-start.8
  20.0 92.0 %all-reduce.15.cloned.1.call-start = ((), (), s32[]{:S(2)}) async-start(), calls=%async_computation.1 | async-start | bytes 1048576 | tf_op jit(solution)/shard_map/psum | solution.py:80
  59.7 4.5 collective-permute-start
  64.3 0.8 copy-start.9
  65.1 100.1 %all-reduce.17.cloned.1.call-start = ((), (), s32[]{:S(2)}) async-start(), calls=%async_computation.2 | async-start | bytes 1048576 | tf_op jit(solution)/shard_map/psum | solution.py:80
  113.0 4.5 collective-permute-start.1
  117.6 0.8 copy-start.10
  118.4 268.6 %all-reduce.33.cloned.1.call-start = ((), (), s32[]{:S(2)}) async-start(), calls=%async_computation.10 | async-start | bytes 16777216 | tf_op jit(solution)/shard_map/psum | solution.py:87
  166.3 14.1 %collective-permute-start.2 = (bf16[128,1024]{1,0:T(8,128)(2,1)S(1)}, bf16[128,1024]{1,0:T(8,128)(2,1)S(1)}, u32[]{:S(2)}, u32[]{:S(2)}) collective-permute-start(bf16[128,1024]{1,0:T(8,128)(2,1)S(1)} %add_convert_fusion.6), channel_id=1, source_target_pairs={{1,0},{2,1},{3,2},{5,4},{6,5},{7,6},{9,8},{10,9},{11,10},{13,12},{... | collective-permute-start | bytes 786440 | tf_op jit(solution)/shard_map/ppermute | solution.py:82
  180.4 5.2 copy-start.5
  188.4 1.1 copy-start.17
  188.4 312.2 %all-reduce.19.cloned.1.call-start = ((), (), s32[]{:S(2)}) async-start(), calls=%async_computation.3 | async-start | bytes 1048576 | tf_op jit(solution)/shard_map/psum | solution.py:126
  387.1 6.0 copy-start.6
  408.2 5.6 collective-permute-start.3
  415.8 3.2 collective-permute-start.4
  420.4 4.9 collective-permute-start.5
  426.7 5.0 copy-start
  431.7 3.7 copy-start.1
  435.4 3.7 copy-start.2
  439.1 3.7 copy-start.3
  442.8 3.7 copy-start.4
  448.6 0.8 copy-start.11
  449.4 135.8 %all-reduce.21.cloned.1.call-start = ((), (), s32[]{:S(2)}) async-start(), calls=%async_computation.4 | async-start | bytes 1048576 | tf_op jit(solution)/shard_map/psum | solution.py:126
  501.7 5.9 collective-permute-start.9
  503.0 4.6 collective-permute-start.6
  508.4 0.8 copy-start.12
  509.2 162.7 %all-reduce.23.cloned.1.call-start = ((), (), s32[]{:S(2)}) async-start(), calls=%async_computation.5 | async-start | bytes 1048576 | tf_op jit(solution)/shard_map/psum | solution.py:126
  586.4 5.9 collective-permute-start.10
  587.7 4.6 collective-permute-start.7
  593.1 0.8 copy-start.13
  593.9 160.9 %all-reduce.25.cloned.1.call-start = ((), (), s32[]{:S(2)}) async-start(), calls=%async_computation.6 | async-start | bytes 1048576 | tf_op jit(solution)/shard_map/psum | solution.py:126
  673.1 41.2 %collective-permute-start.11 = (bf16[128,1024]{1,0:T(8,128)(2,1)S(1)}, bf16[128,1024]{1,0:T(8,128)(2,1)S(1)}, u32[]{:S(2)}, u32[]{:S(2)}) collective-permute-start(bf16[128,1024]{1,0:T(8,128)(2,1)S(1)} %add_convert_fusion.3), channel_id=1, source_target_pairs={{0,1},{1,2},{2,3},{4,5},{5,6},{6,7},{8,9},{9,10},{10,11},{12,13},{... | collective-permute-start | bytes 786440 | tf_op jit(solution)/shard_map/ppermute | solution.py:131
  674.4 4.6 collective-permute-start.8
  716.8 0.8 copy-start.14
  717.6 87.7 %all-reduce.27.cloned.1.call-start = ((), (), s32[]{:S(2)}) async-start(), calls=%async_computation.7 | async-start | bytes 1048576 | tf_op jit(solution)/shard_map/psum | solution.py:126
  755.9 4.4 collective-permute-start.12
  762.8 0.8 copy-start.15
  763.6 89.8 %all-reduce.29.cloned.1.call-start = ((), (), s32[]{:S(2)}) async-start(), calls=%async_computation.8 | async-start | bytes 1048576 | tf_op jit(solution)/shard_map/psum | solution.py:126
  806.4 4.4 collective-permute-start.13
  813.3 0.8 copy-start.16
  814.1 75.9 %all-reduce.31.cloned.1.call-start = ((), (), s32[]{:S(2)}) async-start(), calls=%async_computation.9 | async-start | bytes 1572864 | tf_op jit(solution)/shard_map/psum | solution.py:135
Sparse Core Ops, SparseCore 0:
  20.1 38.4 all-reduce.12
  65.2 46.6 all-reduce.14
  118.6 46.5 all-reduce.16
  188.6 198.4 all-reduce.32
  449.5 51.0 all-reduce.18
  509.4 75.7 all-reduce.20
  594.0 77.8 all-reduce.22
  717.7 37.0 all-reduce.24
  763.7 41.5 all-reduce.26
  814.2 39.1 all-reduce.28
  856.4 33.5 all-reduce.30
where the time goes:
time: 904 us; the launch traced here: 899 us
  waiting for transfers between devices  705 us (78%)
  local copies, waits for them, and re-layouts  53.5 us (6%)
  other arithmetic  52.1 us (6%)
  starting transfers between devices  34.7 us (4%)
  matrix products  21.7 us (2%)
  between operations  21 us (2%)
  blocking collectives  10.2 us (1%)
    psum x6, waiting for transfers between devices, device_step(): summed = lax.psum(branch, 'model')  323 us
    psum x1, waiting for transfers between devices, device_step(): mean_up = lax.psum(g_up[0, 0] + grad_up, 'data') / n_data  197 us
    psum x3, waiting for transfers between devices, device_step(): summed = lax.psum(part_sum, 'model')  132 us
    psum x1, waiting for transfers between devices, device_step(): lax.psum(jnp.where(stage_id == n_stage - 1, y_local, jnp.zeros_like(y_loc...  34.4 us
    convert_element_type x1, other arithmetic, apply_update(): down_w.astype(jnp.bfloat16)  24.5 us
    cond x16, local copies, waits for them, and re-layouts  21.8 us
    unnamed x31, local copies, waits for them, and re-layouts  20.1 us
  transfers between devices with their start and end apart: 25, of which 19 were waited for; matrix products, arithmetic and copies ran while one was open for 5% of the time, Pallas kernels for 0%

commit v1 on v0

v1 whole, which is shorter than its diff:
```python
import functools

import jax
import jax.numpy as jnp
from jax import lax
from jax.experimental import pallas as pl
from jax.experimental.pallas import tpu as pltpu
from jax.sharding import PartitionSpec as P

ADAM_STEP = 10
BETA_ONE = 0.9
BETA_TWO = 0.95
ADAM_EPS = 1e-8
WEIGHT_DECAY = 0.1
NORM_EPS = 1e-6
GELU_A = 0.7978845608028654
GELU_B = 0.044715
NT = (((1,), (1,)), ((), ()))
TN = (((0,), (0,)), ((), ()))
MESH = pl.DeviceIdType.MESH
F32 = jnp.float32
BF16 = jnp.bfloat16
NZ = 4
NS = 4
ROWS = 128
D = 1024
QROWS = ROWS // NZ
CH = 128
NCHUNK = 2 * D // CH
R = 64
RQ = R // NZ
NSUB = ROWS // R
NMICRO = 3
NF = NMICRO * 2 * NSUB
PRE = (11, 8, 5, 2)


def gelu_parts(x):
    t = jnp.tanh(GELU_A * (x + GELU_B * (x * x * x)))
    return 0.5 * (1.0 + t), t


def rcopy(src, dst, ssem, rsem, dev):
    return pltpu.make_async_remote_copy(src, dst, ssem, rsem, device_id=dev, device_id_type=MESH)


def axes():
    return lax.axis_index('model'), lax.axis_index('data'), lax.axis_index('stage')


def back_kernel(wu, wd, gu, gd, a_ref, dy_ref, x_ref, mn_ref,
                gbu, gbd, c_ref, xo_ref,
                wf, wub, wdb, gin, gown, fa, fg, fh, fz, gp, part, rsb, gsend, nacc, nsend, nbuf,
                wsem, osem, outsem, cs, cr, fs, fr, rs, rr, gs, gr, xs, xr, ys, yr, ns, nr):
    m, d, s = axes()
    prim = d == lax.rem(s, 2)
    sec = jnp.logical_not(prim)
    peer = (m, 1 - d, s)

    def chunk_copy(c, src):
        row = pl.ds(pl.multiple_of(lax.rem(c, D // CH) * CH, CH), CH)
        return rcopy(src.at[0, 0, row], gin.at[c // (D // CH), row], cs.at[c], cr.at[c], peer)

    def send_chunks(lo, hi):
        half = D // CH

        @pl.loop(lo, jnp.minimum(hi, half))
        def _(c):
            chunk_copy(c, gd).start()

        @pl.loop(jnp.maximum(lo, half), hi)
        def _(c):
            chunk_copy(c, gu).start()

    pre = jnp.where(s == 0, PRE[0], jnp.where(s == 1, PRE[1], jnp.where(s == 2, PRE[2], PRE[3])))
    own = pl.ds(0, ROWS)
    oth = pl.ds(ROWS, ROWS)
    fcopy = [rcopy(a_ref.at[0], fa.at[oth], fs.at[0], fr.at[0], peer)]
    fcopy += [rcopy(f.at[own], f.at[oth], fs.at[i + 1], fr.at[i + 1], peer) for i, f in enumerate((fh, fg, fz))]

    wcopies = [pltpu.make_async_copy(wu.at[0], wf.at[0], wsem.at[0]), pltpu.make_async_copy(wd.at[0], wf.at[1], wsem.at[1])]
    for cp in wcopies:
        cp.start()
    qrow = pl.ds(pl.multiple_of(m * QROWS, QROWS), QROWS)
    xcopy = rcopy(x_ref.at[:, qrow], xo_ref.at[:, qrow], xs.at[0], xr.at[0], (m, 0, s))

    @pl.when(sec)
    def _():
        @pl.when(s == 0)
        def _():
            xcopy.start()
        fcopy[0].start()
        send_chunks(0, pre)

    gcopies = [pltpu.make_async_copy(gd.at[0, 0], gown.at[0], osem.at[0]), pltpu.make_async_copy(gu.at[0, 0], gown.at[1], osem.at[1])]

    @pl.when(prim)
    def _():
        for cp in gcopies:
            cp.start()

    fa[own] = a_ref[0]
    for i, (cp, dst) in enumerate(zip(wcopies, (wub, wdb))):
        cp.wait()

        @pl.loop(0, D // CH)
        def _(c):
            row = pl.ds(pl.multiple_of(c * CH, CH), CH)
            dst[row] = wf[i, row].astype(BF16)
        if i == 0:
            pre_act = jnp.dot(a_ref[0], wub[...], preferred_element_type=F32)
            cdf, t = gelu_parts(pre_act)
            fh[own] = (pre_act * cdf).astype(BF16)
            gp[...] = cdf + pre_act * (0.5 * (1.0 - t * t) * GELU_A * (1.0 + 3.0 * GELU_B * (pre_act * pre_act)))

    @pl.when(sec)
    def _():
        fcopy[1].start()

    xfwd = [rcopy(xo_ref.at[:, qrow], xo_ref.at[:, qrow], ys.at[o - 1], yr.at[o - 1], (lax.rem(m + o, NZ), d, s)) for o in range(1, NZ)]

    @pl.when(jnp.logical_and(s == 0, d == 0))
    def _():
        xcopy.wait_recv()
        for cp in xfwd:
            cp.start()

    gsends = [rcopy(gsend, fg.at[qrow], gs.at[o], gr.at[o], (lax.rem(m + o, NZ), d, s - 1)) for o in range(NZ)]

    @pl.when(s == NS - 1)
    def _():
        fg[own] = dy_ref[...]

    @pl.when(s < NS - 1)
    def _():
        for cp in gsends:
            cp.wait_recv()

    @pl.when(sec)
    def _():
        fcopy[2].start()

    grad_hid = lax.dot_general(fg[own], wdb[...], NT, preferred_element_type=F32)
    fz[own] = (gp[...] * grad_hid).astype(BF16)

    @pl.when(s > 0)
    def _():
        part[...] = lax.dot_general(fz[own], wub[...], NT, preferred_element_type=F32)
        rcp = []
        for o in range(1, NZ):
            to = lax.rem(m + o, NZ)
            row = pl.ds(pl.multiple_of(to * QROWS, QROWS), QROWS)
            rcp.append(rcopy(part.at[row], rsb.at[o - 1], rs.at[o - 1], rr.at[o - 1], (to, d, s)))
        for cp in rcp:
            cp.start()
        total = part[qrow]
        for o, cp in enumerate(rcp):
            cp.wait_recv()
            total = total + rsb[o]
        gsend[...] = (fg[qrow].astype(F32) + total).astype(BF16)
        for cp in gsends:
            cp.start()
        for cp in rcp:
            cp.wait_send()

    @pl.when(sec)
    def _():
        fcopy[3].start()
        send_chunks(pre, NCHUNK)

    @pl.when(s > 0)
    def _():
        for cp in gsends:
            cp.wait_send()

    slot = s * NZ + m

    @pl.when(prim)
    def _():
        for cp in gcopies:
            cp.wait()
        for cp in fcopy:
            cp.wait_recv()
        nacc[...] = jnp.zeros_like(nacc)
        for half, (lhs, rhs, src, out) in enumerate(((fh, fg, gd, gbd), (fa, fz, gu, gbu))):
            @pl.loop(0, D // CH)
            def _(c):
                row = pl.ds(pl.multiple_of(c * CH, CH), CH)
                grad = lax.dot_general(lhs[:, row], rhs[...], TN, preferred_element_type=F32)
                chunk_copy(half * (D // CH) + c, src).wait_recv()
                bar = (gown[half, row] + gin[half, row] + grad) * 0.5
                gown[half, row] = bar
                nacc[...] += jnp.sum((bar * bar).reshape(CH // 8, 8, D), axis=0)
                pltpu.make_async_copy(gown.at[half, row], out.at[row], outsem.at[half * (D // CH) + c]).start()
        tot = nacc[:, 0:128]
        for i in range(1, D // 128):
            tot = tot + nacc[:, i * 128:(i + 1) * 128]
        nsend[...] = tot
        nbuf[slot] = tot

    def ncopy(to, sl):
        return rcopy(nsend, nbuf.at[sl], ns.at[to], nr.at[sl], (to // (2 * NS), lax.rem(to // NS, 2), lax.rem(to, NS)))

    me = (m * 2 + d) * NS + s

    @pl.when(prim)
    def _():
        @pl.loop(0, NZ * 2 * NS)
        def _(to):
            @pl.when(to != me)
            def _():
                ncopy(to, slot).start()

    @pl.loop(0, NZ * NS)
    def _(i):
        @pl.when(jnp.logical_or(sec, i != slot))
        def _():
            ncopy(0, i).wait_recv()

    total = jnp.sum(jnp.sum(nbuf[...], axis=0), keepdims=True)
    c_ref[...] = jnp.broadcast_to(jnp.minimum(1.0, mn_ref[0] / (jnp.sqrt(total) + NORM_EPS)), c_ref.shape)

    @pl.when(prim)
    def _():
        @pl.loop(0, NZ * 2 * NS)
        def _(to):
            @pl.when(to != me)
            def _():
                ncopy(to, slot).wait_send()
        for half, out in enumerate((gbd, gbu)):
            @pl.loop(0, D // CH)
            def _(c):
                row = pl.ds(pl.multiple_of(c * CH, CH), CH)
                pltpu.make_async_copy(gown.at[half, row], out.at[row], outsem.at[half * (D // CH) + c]).wait()

    @pl.when(sec)
    def _():
        for cp in fcopy:
            cp.wait_send()

        @pl.loop(0, NCHUNK)
        def _(c):
            chunk_copy(c, gd).wait_send()

    @pl.when(jnp.logical_and(s == 0, d == 0))
    def _():
        for cp in xfwd:
            cp.wait()

    @pl.when(jnp.logical_and(s == 0, d == 1))
    def _():
        xcopy.wait_send()


def fwd_kernel(w1, w2, x_ref, xo_ref, gbu_in, gbd_in, gbu, gbd, y_ref,
               inb, part, rsb, osend, isem, ir, rs, rr, os, yl, ys, yr, cs, cr):
    m, d, s = axes()
    prim = d == lax.rem(s, 2)
    sec = jnp.logical_not(prim)
    peer = (m, 1 - d, s)
    half = D // CH
    oq = pl.ds(pl.multiple_of(m * RQ, RQ), RQ)

    def bulk(c, ref):
        row = pl.ds(pl.multiple_of(lax.rem(c, half) * CH, CH), CH)
        return rcopy(ref.at[row], ref.at[row], cs.at[c], cr.at[c], peer)

    def send_chunks(lo, hi):
        @pl.loop(lo, jnp.minimum(hi, half))
        def _(c):
            bulk(c, gbd).start()

        @pl.loop(jnp.maximum(lo, half), hi)
        def _(c):
            bulk(c, gbu).start()

    up = 1 + 2 * s

    def goal(k):
        return up + (NCHUNK - up) * k // NF

    def where_is(k):
        return k // (2 * NSUB), lax.rem(k // NSUB, 2), lax.rem(k, NSUB)

    def in_copy(k, o):
        return rcopy(osend.at[k], inb.at[k, oq], os.at[k, o], ir.at[k, o], (lax.rem(m + o, NZ), lax.rem(s + 1, 2), s + 1))

    def rs_copy(k, o):
        to = lax.rem(m + o, NZ)
        row = pl.ds(pl.multiple_of(to * RQ, RQ), RQ)
        return rcopy(part.at[k, row], rsb.at[k, o - 1], rs.at[k, o - 1], rr.at[k, o - 1], (to, d, s))

    def y_place(k):
        i, r, sub = where_is(k)
        return i, r, i * NSUB + sub, pl.ds(pl.multiple_of(sub * R + m * RQ, RQ), RQ)

    def y_copy(k, o, st):
        i, r, kk, row = y_place(k)
        return rcopy(osend.at[k], y_ref.at[i, row], ys.at[k, o * NS + st], yr.at[kk, o], (lax.rem(m + o, NZ), r, st))

    def y_local(k):
        i, r, kk, row = y_place(k)
        return pltpu.make_async_copy(osend.at[k], y_ref.at[i, row], yl.at[k])

    def is_self(k, o, st):
        r = lax.rem(k // NSUB, 2)
        return jnp.logical_and(r == d, (o == 0) and (st == NS - 1))

    def compute(k):
        @pl.when(s > 0)
        def _():
            for o in range(NZ):
                in_copy(k, o).wait_recv()
        pre_act = jnp.dot(inb[k], w1[...], preferred_element_type=F32)
        hid = (pre_act * gelu_parts(pre_act)[0]).astype(BF16)
        part[k] = jnp.dot(hid, w2[...], preferred_element_type=F32)
        for o in range(1, NZ):
            rs_copy(k, o).start()

    def finish(k):
        total = part[k, oq]
        for o in range(1, NZ):
            rs_copy(k, o).wait_recv()
            total = total + rsb[k, o - 1]
        osend[k] = (inb[k, oq].astype(F32) + total).astype(BF16)

        @pl.when(s < NS - 1)
        def _():
            for o in range(NZ):
                in_copy(k, o).start()

        @pl.when(s == NS - 1)
        def _():
            for o in range(NZ):
                for st in range(NS):
                    if o == 0 and st == NS - 1:
                        @pl.when(is_self(k, o, st))
                        def _():
                            y_local(k).start()

                        @pl.when(jnp.logical_not(is_self(k, o, st)))
                        def _():
                            y_copy(k, o, st).start()
                    else:
                        y_copy(k, o, st).start()

    def in_local(k, src, row, i):
        return pltpu.make_async_copy(src.at[i, row], inb.at[k], isem.at[k])

    @pl.when(prim)
    def _():
        @pl.when(s == 0)
        def _():
            for step in ('start', 'wait'):
                for k in range(NF):
                    i, r, sub = k // (2 * NSUB), (k // NSUB) % 2, k % NSUB
                    getattr(in_local(k, (x_ref, xo_ref)[r], pl.ds(sub * R, R), i), step)()
        send_chunks(0, up)
        compute(0)

        @pl.loop(1, NF)
        def _(k):
            compute(k)
            finish(k - 1)
            send_chunks(goal(k - 1), goal(k))
        finish(NF - 1)
        send_chunks(goal(NF - 1), NCHUNK)

    @pl.loop(0, NF // 2)
    def _(kk):
        i, sub = kk // NSUB, lax.rem(kk, NSUB)
        k = i * 2 * NSUB + d * NSUB + sub
        for o in range(NZ):
            mine = jnp.logical_and(jnp.logical_and(s == NS - 1, prim), o == 0)

            @pl.when(jnp.logical_not(mine))
            def _():
                y_copy(k, o, 0).wait_recv()

            if o == 0:
                @pl.when(mine)
                def _():
                    y_local(k).wait()

    @pl.when(sec)
    def _():
        @pl.loop(0, NCHUNK)
        def _(c):
            bulk(c, gbd).wait_recv()

    @pl.when(prim)
    def _():
        @pl.loop(0, NF)
        def _(k):
            for o in range(1, NZ):
                rs_copy(k, o).wait_send()

            @pl.when(s < NS - 1)
            def _():
                for o in range(NZ):
                    in_copy(k, o).wait_send()

            @pl.when(s == NS - 1)
            def _():
                for o in range(NZ):
                    for st in range(NS):
                        if o == 0 and st == NS - 1:
                            @pl.when(jnp.logical_not(is_self(k, o, st)))
                            def _():
                                y_copy(k, o, st).wait_send()
                        else:
                            y_copy(k, o, st).wait_send()

        @pl.loop(0, NCHUNK)
        def _(c):
            bulk(c, gbd).wait_send()


def adamw_update(weight, moment_one, moment_two, grad_step, step_rate):
    mom_new = BETA_ONE * moment_one + (1.0 - BETA_ONE) * grad_step
    sec_new = BETA_TWO * moment_two + (1.0 - BETA_TWO) * grad_step * grad_step
    one_corr = 1.0 - BETA_ONE ** ADAM_STEP
    two_corr = 1.0 - BETA_TWO ** ADAM_STEP
    direction = (mom_new / one_corr) / (jnp.sqrt(sec_new / two_corr) + ADAM_EPS)
    weight_new = weight - step_rate * (direction + WEIGHT_DECAY * weight)
    return weight_new, mom_new, sec_new


def solution(mesh):
    up_spec = P('stage', None, 'model')
    down_spec = P('stage', 'model', None)
    row_spec = P(None, 'data', None)
    in_specs = (up_spec, down_spec, up_spec, down_spec, up_spec, down_spec, P('data', 'stage', None, 'model'), P('data', 'stage', 'model', None), P('stage', 'data', None), P('data', None), row_spec, P(None), P(None))
    out_specs = (up_spec, down_spec, up_spec, down_spec, up_spec, down_spec, row_spec)
    hbm = pl.BlockSpec(memory_space=pl.ANY)
    vm = pl.BlockSpec(memory_space=pltpu.VMEM)
    sm = pl.BlockSpec(memory_space=pltpu.SMEM)
    dma = pltpu.SemaphoreType.DMA
    mat = jax.ShapeDtypeStruct((D, D), F32)

    def device_step(w_up, w_down, m_up, m_down, v_up, v_down, g_up, g_down, acts_last, grad_out, x_next, learn_rate, max_norm):
        gbu, gbd, clip, x_other = pl.pallas_call(
            back_kernel,
            name='back',
            out_shape=(mat, mat, jax.ShapeDtypeStruct((8, 128), F32), jax.ShapeDtypeStruct((NMICRO, ROWS, D), BF16)),
            in_specs=[hbm, hbm, hbm, hbm, vm, vm, hbm, sm],
            out_specs=(hbm, hbm, vm, hbm),
            scratch_shapes=[
                pltpu.VMEM((2, D, D), F32), pltpu.VMEM((D, D), BF16), pltpu.VMEM((D, D), BF16),
                pltpu.VMEM((2, D, D), F32), pltpu.VMEM((2, D, D), F32),
                *[pltpu.VMEM((2 * ROWS, D), BF16)] * 4,
                pltpu.VMEM((ROWS, D), F32), pltpu.VMEM((ROWS, D), F32), pltpu.VMEM((NZ - 1, QROWS, D), F32),
                pltpu.VMEM((QROWS, D), BF16), pltpu.VMEM((8, D), F32), pltpu.VMEM((8, 128), F32), pltpu.VMEM((NZ * NS, 8, 128), F32),
                dma((2,)), dma((2,)), dma((NCHUNK,)), dma((NCHUNK,)), dma((NCHUNK,)), dma((4,)), dma((4,)),
                dma((NZ - 1,)), dma((NZ - 1,)), dma((NZ,)), dma((NZ,)), dma((1,)), dma((1,)), dma((NZ - 1,)), dma((NZ - 1,)),
                dma((NZ * 2 * NS,)), dma((NZ * NS,)),
            ],
            compiler_params=pltpu.CompilerParams(has_side_effects=True, vmem_limit_bytes=48 << 20),
        )(w_up, w_down, g_up, g_down, acts_last, grad_out, x_next, max_norm)
        clip = clip[0, 0]
        rate = learn_rate[0]
        up_bf = adamw_update(w_up[0], m_up[0], v_up[0], clip * gbu, rate)[0].astype(BF16)
        down_bf = adamw_update(w_down[0], m_down[0], v_down[0], clip * gbd, rate)[0].astype(BF16)
        gbu, gbd, y = pl.pallas_call(
            fwd_kernel,
            name='fwd',
            out_shape=(mat, mat, jax.ShapeDtypeStruct((NMICRO, ROWS, D), BF16)),
            in_specs=[vm, vm, hbm, hbm, hbm, hbm],
            out_specs=(hbm, hbm, hbm),
            scratch_shapes=[
                pltpu.VMEM((NF, R, D), BF16), pltpu.VMEM((NF, R, D), F32), pltpu.VMEM((NF, NZ - 1, RQ, D), F32), pltpu.VMEM((NF, RQ, D), BF16),
                dma((NF,)), dma((NF, NZ)), dma((NF, NZ - 1)), dma((NF, NZ - 1)), dma((NF, NZ)), dma((NF,)), dma((NF, NZ * NS)), dma((NF // 2, NZ)),
                dma((NCHUNK,)), dma((NCHUNK,)),
            ],
            input_output_aliases={4: 0, 5: 1},
            compiler_params=pltpu.CompilerParams(has_side_effects=True, vmem_limit_bytes=20 << 20),
        )(up_bf, down_bf, x_next, x_other, gbu, gbd)
        up_w, up_m, up_v = adamw_update(w_up[0], m_up[0], v_up[0], clip * gbu, rate)
        down_w, down_m, down_v = adamw_update(w_down[0], m_down[0], v_down[0], clip * gbd, rate)
        return (up_w[None], down_w[None], up_m[None], down_m[None], up_v[None], down_v[None], y)

    return jax.shard_map(device_step, mesh=mesh, in_specs=in_specs, out_specs=out_specs, check_vma=False)
```

time: 904 us -> 337 us (0.37)
  waiting for transfers between devices: 705 us -> 0 us
  Pallas kernels: 0 us -> 292 us
  local copies, waits for them, and re-layouts: 53.5 us -> 4.45 us
  starting transfers between devices: 34.7 us -> 0 us
  matrix products: 21.7 us -> 0 us
  between operations: 21 us -> 2.02 us
  other arithmetic: 52.1 us -> 37.2 us
  blocking collectives: 10.2 us -> 0 us
    psum x11 -> x0, waiting for transfers between devices: 686 us -> none  [the longest x6 323 us: device_step(): summed = lax.psum(branch, 'model')]
    pallas_call x0 -> x2, Pallas kernels: none -> 292 us  [the longest x1 172 us: device_step(): pl.pallas_call(fwd_kernel, name='fwd', out_shape=(mat, mat, jax.ShapeDtyp...]
    ppermute x14 -> x0, starting transfers between devices: 34.1 us -> none  [the longest x3 13.5 us: device_step(): incoming = lax.ppermute(norm_acc, 'stage', down_perm)]
    convert_element_type x10 -> x1, other arithmetic: 38.9 us -> 15.5 us  [device_step(): adamw_update(w_down[0], m_down[0], v_down[0], clip * gbd, rate)[0]]
    cond x16 -> x0, local copies, waits for them, and re-layouts: 21.8 us -> none
    dot_general x8 -> x0, matrix products: 21.7 us -> none  [the longest x3 7.32 us: fwd_local(): return jnp.dot(hidden, down_new_bf, preferred_element_type=jnp.float32)]
    broadcast_in_dim x0 -> x2, other arithmetic: none -> 21.7 us  [the longest x1 11.6 us: device_step(): up_v[None]]
    ppermute x14 -> x0, waiting for transfers between devices: 18.6 us -> none  [the longest x3 9.93 us: device_step(): clip_cur = lax.ppermute(clip_cur, 'stage', up_perm)]
  transfers between devices with their start and end apart: 25 -> 0, of which waited for: 19 -> 0; matrix products, arithmetic and copies ran while one was open for 5% -> 0% of each run, Pallas kernels for 0% -> 0%
where the time goes in v1:
time: 337 us; the launch traced here: 335 us
  Pallas kernels  292 us (87%)
  other arithmetic  37.2 us (11%)
  local copies, waits for them, and re-layouts  4.45 us (1%)
    pallas_call x1, Pallas kernels, device_step(): pl.pallas_call(fwd_kernel, name='fwd', out_shape=(mat, mat, jax.ShapeDtyp...  172 us
    pallas_call x1, Pallas kernels, device_step(): pl.pallas_call(back_kernel, name='back', out_shape=(mat, mat, jax.ShapeDt...  120 us
    convert_element_type x1, other arithmetic, device_step(): adamw_update(w_down[0], m_down[0], v_down[0], clip * gbd, rate)[0]  15.5 us
    broadcast_in_dim x1, other arithmetic, device_step(): up_v[None]  11.6 us
    broadcast_in_dim x1, other arithmetic, device_step(): down_v[None]  10.1 us

profile of v1, /device:TPU:7, one launch (start us, length us, event | category | flops | bytes accessed | tf_op | source)
XLA Modules:
  0.0 335.4 jit_solution(13034258440884670899)
XLA Ops:
  1.9 0.0 copy-start.2
  1.9 1.1 copy-done.2
  3.1 0.0 copy-start.4
  3.1 0.9 copy-done.4
  4.0 0.0 copy-start.5
  4.0 0.9 copy-done.5
  5.0 120.0 %back.1 = (f32[1024,1024]{1,0:T(8,128)}, f32[1024,1024]{1,0:T(8,128)}, f32[8,128]{1,0:T(8,128)S(1)}, bf16[3,128,1024]{2,1,0:T(8,128)(2,1)S(1)}) custom-call(f32[1,1024,1024]{2,1,0:T(8,128)} %wu.1, f32[1,1024,1024]{2,1,0:T(8,128)} %wd.1, f32[1,1,1024,1024]{3,2,1,0:T(8,128)} %gu.1, f32[1,1,1024,1024]{3,2,1,0:T(8,128)} %gd.1, ...), custom_call_target="tpu_custom_call" | custom-call | tf_op jit(solution)/shard_map/back/pallas_call | solution.py:442
  124.9 0.5 slice.3
  125.4 0.0 copy-start
  125.4 0.0 copy-start.1
  125.5 0.0 copy-start.3
  125.5 15.5 %fusion.15 = (bf16[1024,1024]{1,0:T(8,128)(2,1)S(1)}, bf16[1024,1024]{1,0:T(8,128)(2,1)S(1)}) fusion(f32[1,1024,1024]{2,1,0:T(8,128)} %wd.1, f32[1024,1024]{1,0:T(8,128)} %get-tuple-element.16.gbd_in, f32[1,1024,1024]{2,1,0:T(8,128)} %param.18, f32[1,1024,1024]{2,1,0:T(8,128)} %param.16, f32[]{:T(128)} %bitcast.3, f32[]{:T(128)} %bitcast.82, ...), kind=kLoop, calls=%fused_computation.24 | loop fusion | flops 35651584 | bytes 37748744 | tf_op jit(solution)/shard_map/convert_element_type | solution.py:463
  140.9 0.0 copy-done
  140.9 0.0 copy-done.1
  140.9 0.0 copy-done.3
  141.0 0.0 copy-start.6
  141.0 171.8 %fwd.1 = (f32[1024,1024]{1,0:T(8,128)S(1)}, f32[1024,1024]{1,0:T(8,128)S(1)}, bf16[3,128,1024]{2,1,0:T(8,128)(2,1)S(1)}) custom-call(bf16[1024,1024]{1,0:T(8,128)(2,1)S(1)} %get-tuple-element.28.w1, bf16[1024,1024]{1,0:T(8,128)(2,1)S(1)} %get-tuple-element.27.w2, bf16[3,128,1024]{2,1,0:T(8,128)(2,1)S(1)} %copy-done.3, ...), custom_call_target="tpu_custom_call", output_to_operand_aliasing={{0}: (4, {}), {1}: (5, {})} | custom-call | tf_op jit(solution)/shard_map/fwd/pallas_call | solution.py:464
  312.8 0.0 copy-done.6
  312.8 0.0 copy-start.7
  312.8 0.0 copy-start.8
  312.8 11.6 %fusion.23 = (f32[1,1024,1024]{2,1,0:T(8,128)}, f32[1,1024,1024]{2,1,0:T(8,128)}, f32[1,1024,1024]{2,1,0:T(8,128)}) fusion(f32[1024,1024]{1,0:T(8,128)S(1)} %get-tuple-element.18, f32[]{:T(128)} %bitcast.3, f32[1,1024,1024]{2,1,0:T(8,128)} %param.17, f32[1,1024,1024]{2,1,0:T(8,128)} %param.15, f32[]{:T(128)} %bitcast.84, f32[1,1024,1024]{2,1,0:T(8,128)S(1)} %copy-done.6), kind=kLoop, calls=%fused_computation.37 | loop fusion | flops 16777216 | bytes 29360136 | tf_op jit(solution)/shard_map/broadcast_in_dim | solution.py:480
  324.4 0.0 copy-done.7
  324.4 0.0 copy-done.8
  324.4 10.1 %fusion.22 = (f32[1,1024,1024]{2,1,0:T(8,128)}, f32[1,1024,1024]{2,1,0:T(8,128)}, f32[1,1024,1024]{2,1,0:T(8,128)}) fusion(f32[1024,1024]{1,0:T(8,128)S(1)} %get-tuple-element.19, f32[]{:T(128)} %bitcast.3, f32[1,1024,1024]{2,1,0:T(8,128)S(1)} %copy-done.8, f32[1,1024,1024]{2,1,0:T(8,128)} %param.16, f32[]{:T(128)} %bitcast.83, f32[1,1024,1024]{2,1,0:T(8,128)S(1)} %copy-done.7), kind=kLoop, calls=%fused_computation.36 | loop fusion | flops 16777216 | bytes 29360136 | tf_op jit(solution)/shard_map/broadcast_in_dim | solution.py:480
  334.5 0.9 copy.27
Async XLA Ops:
  1.9 1.1 copy-start.2
  3.1 0.9 copy-start.4
  4.0 0.9 copy-start.5
  125.4 15.5 %copy-start = (f32[1024,1024]{1,0:T(8,128)S(1)}, f32[1024,1024]{1,0:T(8,128)}, u32[]{:S(2)}) copy-start(f32[1024,1024]{1,0:T(8,128)} %get-tuple-element.15.gbu_in) | copy-start | bytes 12582916
  125.4 15.5 %copy-start.1 = (f32[1024,1024]{1,0:T(8,128)S(1)}, f32[1024,1024]{1,0:T(8,128)}, u32[]{:S(2)}) copy-start(f32[1024,1024]{1,0:T(8,128)} %get-tuple-element.16.gbd_in) | copy-start | bytes 12582916
  125.5 15.5 %copy-start.3 = (bf16[3,128,1024]{2,1,0:T(8,128)(2,1)S(1)}, bf16[3,128,1024]{2,1,0:T(8,128)(2,1)}, u32[]{:S(2)}) copy-start(bf16[3,128,1024]{2,1,0:T(8,128)(2,1)} %x_ref.3) | copy-start | bytes 2359300
  141.0 171.8 %copy-start.6 = (f32[1,1024,1024]{2,1,0:T(8,128)S(1)}, f32[1,1024,1024]{2,1,0:T(8,128)}, u32[]{:S(2)}) copy-start(f32[1,1024,1024]{2,1,0:T(8,128)} %wu.1) | copy-start | bytes 12582916
  312.8 11.6 %copy-start.7 = (f32[1,1024,1024]{2,1,0:T(8,128)S(1)}, f32[1,1024,1024]{2,1,0:T(8,128)}, u32[]{:S(2)}) copy-start(f32[1,1024,1024]{2,1,0:T(8,128)} %wd.1) | copy-start | bytes 12582916
  312.8 11.6 %copy-start.8 = (f32[1,1024,1024]{2,1,0:T(8,128)S(1)}, f32[1,1024,1024]{2,1,0:T(8,128)}, u32[]{:S(2)}) copy-start(f32[1,1024,1024]{2,1,0:T(8,128)} %param.18) | copy-start | bytes 12582916

commit v2 on v1

--- a/solution.py
+++ b/solution.py
@@ -13,6 +13,9 @@
 ADAM_EPS = 1e-8
 WEIGHT_DECAY = 0.1
 NORM_EPS = 1e-6
+ROOT_CORR = (1.0 - BETA_TWO ** ADAM_STEP) ** 0.5
+DIR_SCALE = ROOT_CORR / (1.0 - BETA_ONE ** ADAM_STEP)
+DIR_EPS = ADAM_EPS * ROOT_CORR
 GELU_A = 0.7978845608028654
 GELU_B = 0.044715
 NT = (((1,), (1,)), ((), ()))
@@ -253,7 +256,7 @@
 
 
 def fwd_kernel(w1, w2, x_ref, xo_ref, gbu_in, gbd_in, gbu, gbd, y_ref,
-               inb, part, rsb, osend, isem, ir, rs, rr, os, yl, ys, yr, cs, cr):
+               inb, part, rsb, osend, isem, ir, rs, rr, os, yo, ys, yr, yt, yq, cs, cr):
     m, d, s = axes()
     prim = d == lax.rem(s, 2)
     sec = jnp.logical_not(prim)
@@ -290,21 +293,21 @@
         row = pl.ds(pl.multiple_of(to * RQ, RQ), RQ)
         return rcopy(part.at[k, row], rsb.at[k, o - 1], rs.at[k, o - 1], rr.at[k, o - 1], (to, d, s))
 
-    def y_place(k):
+    def y_at(kk, q):
+        i, sub = kk // NSUB, lax.rem(kk, NSUB)
+        return y_ref.at[i, pl.ds(pl.multiple_of(sub * R + q * RQ, RQ), RQ)]
+
+    def y_out(k, xx):
         i, r, sub = where_is(k)
-        return i, r, i * NSUB + sub, pl.ds(pl.multiple_of(sub * R + m * RQ, RQ), RQ)
-
-    def y_copy(k, o, st):
-        i, r, kk, row = y_place(k)
-        return rcopy(osend.at[k], y_ref.at[i, row], ys.at[k, o * NS + st], yr.at[kk, o], (lax.rem(m + o, NZ), r, st))
-
-    def y_local(k):
-        i, r, kk, row = y_place(k)
-        return pltpu.make_async_copy(osend.at[k], y_ref.at[i, row], yl.at[k])
-
-    def is_self(k, o, st):
-        r = lax.rem(k // NSUB, 2)
-        return jnp.logical_and(r == d, (o == 0) and (st == NS - 1))
+        kk = i * NSUB + sub
+        return rcopy(osend.at[k], y_at(kk, m), yo.at[k, xx], yr.at[kk, 0], (m, r, 2 * xx + 1 - r))
+
+    def y_ring(kk, o):
+        return rcopy(y_at(kk, m), y_at(kk, m), ys.at[kk, o], yr.at[kk, o], (lax.rem(m + o, NZ), d, s))
+
+    def y_mate(kk, o):
+        q = lax.rem(m - o + NZ, NZ)
+        return rcopy(y_at(kk, q), y_at(kk, q), yt.at[kk, o], yq.at[kk, o], (m, d, s + 1 - 2 * lax.rem(s, 2)))
 
     def compute(k):
         @pl.when(s > 0)
@@ -331,18 +334,8 @@
 
         @pl.when(s == NS - 1)
         def _():
-            for o in range(NZ):
-                for st in range(NS):
-                    if o == 0 and st == NS - 1:
-                        @pl.when(is_self(k, o, st))
-                        def _():
-                            y_local(k).start()
-
-                        @pl.when(jnp.logical_not(is_self(k, o, st)))
-                        def _():
-                            y_copy(k, o, st).start()
-                    else:
-                        y_copy(k, o, st).start()
+            for xx in range(2):
+                y_out(k, xx).start()
 
     def in_local(k, src, row, i):
         return pltpu.make_async_copy(src.at[i, row], inb.at[k], isem.at[k])
@@ -366,27 +359,37 @@
         finish(NF - 1)
         send_chunks(goal(NF - 1), NCHUNK)
 
-    @pl.loop(0, NF // 2)
-    def _(kk):
-        i, sub = kk // NSUB, lax.rem(kk, NSUB)
-        k = i * 2 * NSUB + d * NSUB + sub
-        for o in range(NZ):
-            mine = jnp.logical_and(jnp.logical_and(s == NS - 1, prim), o == 0)
-
-            @pl.when(jnp.logical_not(mine))
-            def _():
-                y_copy(k, o, 0).wait_recv()
-
-            if o == 0:
-                @pl.when(mine)
-                def _():
-                    y_local(k).wait()
+    @pl.when(sec)
+    def _():
+        @pl.loop(0, NF // 2)
+        def _(kk):
+            y_ring(kk, 0).wait_recv()
+            for o in range(1, NZ):
+                y_ring(kk, o).start()
+            y_mate(kk, 0).start()
+            for o in range(1, NZ):
+                y_ring(kk, o).wait_recv()
+                y_mate(kk, o).start()
+
+    @pl.when(prim)
+    def _():
+        @pl.loop(0, NF // 2)
+        def _(kk):
+            for o in range(NZ):
+                y_mate(kk, o).wait_recv()
 
     @pl.when(sec)
     def _():
         @pl.loop(0, NCHUNK)
         def _(c):
             bulk(c, gbd).wait_recv()
+
+        @pl.loop(0, NF // 2)
+        def _(kk):
+            for o in range(1, NZ):
+                y_ring(kk, o).wait_send()
+            for o in range(NZ):
+                y_mate(kk, o).wait_send()
 
     @pl.when(prim)
     def _():
@@ -402,14 +405,8 @@
 
             @pl.when(s == NS - 1)
             def _():
-                for o in range(NZ):
-                    for st in range(NS):
-                        if o == 0 and st == NS - 1:
-                            @pl.when(jnp.logical_not(is_self(k, o, st)))
-                            def _():
-                                y_copy(k, o, st).wait_send()
-                        else:
-                            y_copy(k, o, st).wait_send()
+                for xx in range(2):
+                    y_out(k, xx).wait_send()
 
         @pl.loop(0, NCHUNK)
         def _(c):
@@ -419,9 +416,7 @@
 def adamw_update(weight, moment_one, moment_two, grad_step, step_rate):
     mom_new = BETA_ONE * moment_one + (1.0 - BETA_ONE) * grad_step
     sec_new = BETA_TWO * moment_two + (1.0 - BETA_TWO) * grad_step * grad_step
-    one_corr = 1.0 - BETA_ONE ** ADAM_STEP
-    two_corr = 1.0 - BETA_TWO ** ADAM_STEP
-    direction = (mom_new / one_corr) / (jnp.sqrt(sec_new / two_corr) + ADAM_EPS)
+    direction = (DIR_SCALE * mom_new) / (jnp.sqrt(sec_new) + DIR_EPS)
     weight_new = weight - step_rate * (direction + WEIGHT_DECAY * weight)
     return weight_new, mom_new, sec_new
 
@@ -466,10 +461,10 @@
             name='fwd',
             out_shape=(mat, mat, jax.ShapeDtypeStruct((NMICRO, ROWS, D), BF16)),
             in_specs=[vm, vm, hbm, hbm, hbm, hbm],
-            out_specs=(hbm, hbm, hbm),
+            out_specs=(hbm, hbm, vm),
             scratch_shapes=[
                 pltpu.VMEM((NF, R, D), BF16), pltpu.VMEM((NF, R, D), F32), pltpu.VMEM((NF, NZ - 1, RQ, D), F32), pltpu.VMEM((NF, RQ, D), BF16),
-                dma((NF,)), dma((NF, NZ)), dma((NF, NZ - 1)), dma((NF, NZ - 1)), dma((NF, NZ)), dma((NF,)), dma((NF, NZ * NS)), dma((NF // 2, NZ)),
+                dma((NF,)), dma((NF, NZ)), dma((NF, NZ - 1)), dma((NF, NZ - 1)), dma((NF, NZ)), dma((NF, 2)), *[dma((NF // 2, NZ))] * 4,
                 dma((NCHUNK,)), dma((NCHUNK,)),
             ],
             input_output_aliases={4: 0, 5: 1},

time: 337 us -> 315 us (0.935)
  Pallas kernels: 292 us -> 270 us
    pallas_call x1, Pallas kernels: 172 us -> 151 us  [device_step(): pl.pallas_call(fwd_kernel, name='fwd', out_shape=(mat, mat, jax.ShapeDtyp...]
where the time goes in v2:
time: 315 us; the launch traced here: 312 us
  Pallas kernels  270 us (86%)
  other arithmetic  35.4 us (11%)
  local copies, waits for them, and re-layouts  4.45 us (1%)
    pallas_call x1, Pallas kernels, device_step(): pl.pallas_call(fwd_kernel, name='fwd', out_shape=(mat, mat, jax.ShapeDtyp...  151 us
    pallas_call x1, Pallas kernels, device_step(): pl.pallas_call(back_kernel, name='back', out_shape=(mat, mat, jax.ShapeDt...  120 us
    convert_element_type x1, other arithmetic, device_step(): adamw_update(w_down[0], m_down[0], v_down[0], clip * gbd, rate)[0]  15 us
    broadcast_in_dim x1, other arithmetic, device_step(): up_v[None]  10.8 us
    broadcast_in_dim x1, other arithmetic, device_step(): down_v[None]  9.5 us

profile of v2, /device:TPU:7, one launch (start us, length us, event | category | flops | bytes accessed | tf_op | source)
XLA Modules:
  0.0 312.3 jit_solution(1882148075481306482)
XLA Ops:
  1.9 0.0 copy-start.2
  1.9 1.1 copy-done.2
  3.1 0.0 copy-start.4
  3.1 0.9 copy-done.4
  4.0 0.0 copy-start.5
  4.0 0.9 copy-done.5
  5.0 120.0 %back.1 = (f32[1024,1024]{1,0:T(8,128)}, f32[1024,1024]{1,0:T(8,128)}, f32[8,128]{1,0:T(8,128)S(1)}, bf16[3,128,1024]{2,1,0:T(8,128)(2,1)S(1)}) custom-call(f32[1,1024,1024]{2,1,0:T(8,128)} %wu.1, f32[1,1024,1024]{2,1,0:T(8,128)} %wd.1, f32[1,1,1024,1024]{3,2,1,0:T(8,128)} %gu.1, f32[1,1,1024,1024]{3,2,1,0:T(8,128)} %gd.1, ...), custom_call_target="tpu_custom_call" | custom-call | tf_op jit(solution)/shard_map/back/pallas_call | solution.py:437
  124.9 0.5 slice.3
  125.4 0.0 copy-start
  125.4 0.0 copy-start.1
  125.5 0.0 copy-start.3
  125.5 15.0 %fusion.24 = (bf16[1024,1024]{1,0:T(8,128)(2,1)S(1)}, bf16[1024,1024]{1,0:T(8,128)(2,1)S(1)}) fusion(f32[1024,1024]{1,0:T(8,128)} %get-tuple-element.16.gbd_in, f32[1,1024,1024]{2,1,0:T(8,128)} %wd.1, f32[1,1024,1024]{2,1,0:T(8,128)} %param.18, f32[1,1024,1024]{2,1,0:T(8,128)} %param.16, f32[]{:T(128)} %bitcast.3, f32[]{:T(128)} %bitcast.90, ...), kind=kLoop, calls=%fused_computation.36 | loop fusion | flops 33554432 | bytes 37748744 | tf_op jit(solution)/shard_map/convert_element_type | solution.py:458
  140.5 0.0 copy-done
  140.5 0.0 copy-done.1
  140.5 0.0 copy-done.3
  140.5 0.0 copy-start.6
  140.5 150.5 %fwd.1 = (f32[1024,1024]{1,0:T(8,128)S(1)}, f32[1024,1024]{1,0:T(8,128)S(1)}, bf16[3,128,1024]{2,1,0:T(8,128)(2,1)S(1)}) custom-call(bf16[1024,1024]{1,0:T(8,128)(2,1)S(1)} %get-tuple-element.28.w1, bf16[1024,1024]{1,0:T(8,128)(2,1)S(1)} %get-tuple-element.27.w2, bf16[3,128,1024]{2,1,0:T(8,128)(2,1)S(1)} %copy-done.3, ...), custom_call_target="tpu_custom_call", output_to_operand_aliasing={{0}: (4, {}), {1}: (5, {})} | custom-call | tf_op jit(solution)/shard_map/fwd/pallas_call | solution.py:459
  291.0 0.0 copy-done.6
  291.1 0.0 copy-start.7
  291.1 0.0 copy-start.8
  291.1 10.8 %fusion.29 = (f32[1,1024,1024]{2,1,0:T(8,128)}, f32[1,1024,1024]{2,1,0:T(8,128)}, f32[1,1024,1024]{2,1,0:T(8,128)}) fusion(f32[1024,1024]{1,0:T(8,128)S(1)} %get-tuple-element.18, f32[]{:T(128)} %bitcast.3, f32[1,1024,1024]{2,1,0:T(8,128)} %param.17, f32[1,1024,1024]{2,1,0:T(8,128)} %param.15, f32[]{:T(128)} %bitcast.92, f32[1,1024,1024]{2,1,0:T(8,128)S(1)} %copy-done.6), kind=kLoop, calls=%fused_computation.41 | loop fusion | flops 15728640 | bytes 29360136 | tf_op jit(solution)/shard_map/broadcast_in_dim | solution.py:475
  301.9 0.0 copy-done.7
  301.9 0.0 copy-done.8
  301.9 9.5 %fusion.28 = (f32[1,1024,1024]{2,1,0:T(8,128)}, f32[1,1024,1024]{2,1,0:T(8,128)}, f32[1,1024,1024]{2,1,0:T(8,128)}) fusion(f32[1024,1024]{1,0:T(8,128)S(1)} %get-tuple-element.19, f32[]{:T(128)} %bitcast.3, f32[1,1024,1024]{2,1,0:T(8,128)S(1)} %copy-done.8, f32[1,1024,1024]{2,1,0:T(8,128)} %param.16, f32[]{:T(128)} %bitcast.91, f32[1,1024,1024]{2,1,0:T(8,128)S(1)} %copy-done.7), kind=kLoop, calls=%fused_computation.40 | loop fusion | flops 15728640 | bytes 29360136 | tf_op jit(solution)/shard_map/broadcast_in_dim | solution.py:475
  311.4 0.9 copy.27
Async XLA Ops:
  1.9 1.1 copy-start.2
  3.1 0.9 copy-start.4
  4.0 0.9 copy-start.5
  125.4 15.0 %copy-start = (f32[1024,1024]{1,0:T(8,128)S(1)}, f32[1024,1024]{1,0:T(8,128)}, u32[]{:S(2)}) copy-start(f32[1024,1024]{1,0:T(8,128)} %get-tuple-element.15.gbu_in) | copy-start | bytes 12582916
  125.4 15.0 %copy-start.1 = (f32[1024,1024]{1,0:T(8,128)S(1)}, f32[1024,1024]{1,0:T(8,128)}, u32[]{:S(2)}) copy-start(f32[1024,1024]{1,0:T(8,128)} %get-tuple-element.16.gbd_in) | copy-start | bytes 12582916
  125.5 15.1 %copy-start.3 = (bf16[3,128,1024]{2,1,0:T(8,128)(2,1)S(1)}, bf16[3,128,1024]{2,1,0:T(8,128)(2,1)}, u32[]{:S(2)}) copy-start(bf16[3,128,1024]{2,1,0:T(8,128)(2,1)} %x_ref.3) | copy-start | bytes 2359300
  140.5 150.5 %copy-start.6 = (f32[1,1024,1024]{2,1,0:T(8,128)S(1)}, f32[1,1024,1024]{2,1,0:T(8,128)}, u32[]{:S(2)}) copy-start(f32[1,1024,1024]{2,1,0:T(8,128)} %wu.1) | copy-start | bytes 12582916
  291.1 10.9 %copy-start.7 = (f32[1,1024,1024]{2,1,0:T(8,128)S(1)}, f32[1,1024,1024]{2,1,0:T(8,128)}, u32[]{:S(2)}) copy-start(f32[1,1024,1024]{2,1,0:T(8,128)} %wd.1) | copy-start | bytes 12582916
  291.1 10.9 %copy-start.8 = (f32[1,1024,1024]{2,1,0:T(8,128)S(1)}, f32[1,1024,1024]{2,1,0:T(8,128)}, u32[]{:S(2)}) copy-start(f32[1,1024,1024]{2,1,0:T(8,128)} %param.18) | copy-start | bytes 12582916
